TPU v7x, 128 devices: a whole 4x4x4 slice. The times are simulated.
128 devices in a mesh: row: 16 (over x, z), col: 8 (over y, core).
Axes of the slice: x: 4, y: 4, z: 4, core: 2. Of those that a mesh axis runs over, the one named last changes fastest.
Arguments:
- front: float32 [9216, 9216], P('row', 'col')
- child_tiles: float32 [16384, 4096], P(('row', 'col')), may hold values from -0.4375 to 0.4375
- tile_target: int32 [16384], P(('row', 'col')), may hold values from 0 to 20735, as said below
- tile_count: int32 [512], P(('row', 'col')), may hold values from 24 to 32
- probe: float32 [9216, 512], P('col'), may hold values from -1.75 to 1.75
Outputs:
- panel_factor: float32 [9216, 1024], P('row', 'col')
- sketch: float32 [9216, 512], P('row', 'col')
Inputs may be any that keep to these rules, and one draw needn't show every extreme that they name: `tile_target`: among the 128 slots of one device, live or not, each counted once at its target tile and once at the mirrored tile, at most 2 placements fall inside the block of the front held by any one device.
All inputs are finite; a program needn't handle non-finite values.
Results may differ from a plain program's by a relative error of at most 0.00015.
Values sent between devices are 32-bit elements; how exact they have to be, the bound alone decides.
A program may use at most 128 MiB of HBM per device.

v0:
```python
import jax
import jax.numpy as jnp
from jax import lax
from jax.sharding import PartitionSpec as P

NB = 512
PANELS = 2
TB = 64
SLOTS = 32
HIGH = lax.Precision.HIGHEST


def in_blocks(value, dim, size):
    before, after = (value.shape[:dim], value.shape[dim + 1 :])
    return jnp.moveaxis(value.reshape(*before, size, -1, *after), dim, 0)


def joined_along(tiles, dim):
    lengths = list(tiles.shape[1:])
    lengths[dim] *= tiles.shape[0]
    return jnp.moveaxis(tiles, 0, dim).reshape(lengths)


def one_exchange(value, axis, axes, splits, concats):
    sizes = [lax.axis_size(a) for a in axes]
    tiles = in_blocks(value, splits[0], sizes[0])
    tiles = jnp.moveaxis(in_blocks(tiles, splits[1] + 1, sizes[1]), 0, 1)
    inside = tiles.shape[2:]
    tiles = tiles.reshape(-1, *inside)
    tiles = lax.all_to_all(tiles, axis, split_axis=0, concat_axis=0, tiled=True)
    tiles = joined_along(tiles.reshape(*sizes, *inside), concats[0] + 1)
    return joined_along(tiles, concats[1])


def filled_up(lines, size):
    spare = -lines.shape[0] % size
    if not spare:
        return lines
    return jnp.concatenate([lines, jnp.zeros((spare, *lines.shape[1:]), lines.dtype)])


def from_root(value, axis, root):
    lines = jnp.where(lax.axis_index(axis) == root, value, jnp.zeros_like(value)).reshape(
        -1, *value.shape[1:][-1:]
    )
    padded = filled_up(lines, lax.axis_size(axis))
    own = lax.psum_scatter(padded, axis, scatter_dimension=0, tiled=True)
    return lax.all_gather(own, axis, axis=0, tiled=True)[: len(lines)].reshape(value.shape)


def broadcast(value, axis, root):
    mine = lax.axis_index(axis) == root
    return lax.psum(jnp.where(mine, value, jnp.zeros_like(value)), axis)


def sum_at_owner(value, axis, dim):
    tiles = in_blocks(value, dim, lax.axis_size(axis))
    arrived = lax.all_to_all(tiles, axis, split_axis=0, concat_axis=0, tiled=True)
    return arrived.sum(axis=0)


def per_device(front, child_tiles, tile_target, tile_count, probe):
    row_count = lax.axis_size("row")
    col_count = lax.axis_size("col")
    devices = row_count * col_count
    local_rows, local_cols = front.shape
    tile_rows = local_rows // TB
    tile_cols = local_cols // TB
    grid = tile_cols * col_count
    local_tiles = tile_rows * tile_cols
    held = child_tiles.shape[0]
    capacity = 2 * max(1, (held + devices - 1) // devices)
    slot_index = jnp.arange(held, dtype=jnp.int32)
    live_once = slot_index % SLOTS < tile_count[slot_index // SLOTS]
    live = jnp.concatenate([live_once, live_once])
    mirrored = child_tiles.reshape(held, TB, TB).transpose(0, 2, 1).reshape(held, TB * TB)
    placements = jnp.concatenate([child_tiles, mirrored], axis=0)
    first_row = tile_target // grid
    first_col = tile_target % grid
    target_row = jnp.concatenate([first_row, first_col])
    target_col = jnp.concatenate([first_col, first_row])
    owner = target_row // tile_rows * col_count + target_col // tile_cols
    place = target_row % tile_rows * tile_cols + target_col % tile_cols
    onehot = (
        (owner[:, None] == jnp.arange(devices, dtype=jnp.int32)[None, :]) & live[:, None]
    ).astype(jnp.int32)
    earlier = jnp.cumsum(onehot, axis=0) - onehot
    rank = jnp.sum(earlier * onehot, axis=1)
    slot = jnp.where(live, owner * capacity + rank, devices * capacity)
    outgoing = (
        jnp.zeros((devices * capacity + 1, TB * TB), jnp.float32).at[slot].set(placements)[:-1]
    )
    where_to = jnp.full((devices * capacity + 1,), local_tiles, jnp.int32).at[slot].set(place)[:-1]
    shaped = (
        outgoing.reshape(row_count, col_count * capacity, TB * TB),
        where_to.reshape(row_count, col_count * capacity),
    )
    incoming, landing = (
        one_exchange(shaped[0], ("row", "col"), ("row", "col"), (0, 1), (0, 1)),
        one_exchange(shaped[1], ("row", "col"), ("row", "col"), (0, 1), (0, 1)),
    )
    incoming = incoming.reshape(-1, TB * TB)
    landing = landing.reshape(-1)
    extend = (
        jnp.zeros((local_tiles + 1, TB * TB), jnp.float32).at[landing].add(incoming)[:local_tiles]
    )
    extend = (
        extend.reshape(tile_rows, tile_cols, TB, TB)
        .transpose(0, 2, 1, 3)
        .reshape(local_rows, local_cols)
    )
    matrix = front + extend
    row_start = lax.axis_index("row") * local_rows
    col_start = lax.axis_index("col") * local_cols
    global_rows = row_start + jnp.arange(local_rows, dtype=jnp.int32)
    group = row_count // col_count
    margin = jnp.zeros((NB, NB), jnp.float32)
    factor_parts = []
    for k in range(PANELS):
        low = k * NB
        high = low + NB
        owner_col = low // local_cols
        offset = low % local_cols
        panel = from_root(matrix[:, offset : offset + NB], "col", owner_col)
        padded = jnp.concatenate([margin, panel, margin], axis=0)
        begin = jnp.clip(low - row_start + NB, 0, local_rows + NB)
        piece = lax.dynamic_slice_in_dim(padded, begin, NB, 0)
        diag_block = lax.psum(piece, "row")
        chol = jnp.linalg.cholesky(0.5 * (diag_block + diag_block.T))
        solved = jax.scipy.linalg.solve_triangular(chol, panel.T, lower=True).T
        factor_parts.append(jnp.where((global_rows >= low)[:, None], solved, 0.0))
        trail = jnp.where((global_rows >= high)[:, None], solved, 0.0)
        column_owner = lax.axis_index("col") * group
        pieces = [broadcast(trail, "row", column_owner + member) for member in range(group)]
        across = jnp.concatenate(pieces, axis=0)
        matrix = matrix - jnp.dot(trail, across.T, precision=HIGH)
    start = PANELS * NB
    global_cols = col_start + jnp.arange(local_cols, dtype=jnp.int32)
    weighted = jnp.where((global_cols >= start)[:, None], probe, 0.0)
    shares = sum_at_owner(
        lax.dot_general(weighted, matrix, (((0,), (1,)), ((), ())), precision=HIGH), "col", 0
    )
    sketch = jnp.where((global_rows >= start)[:, None], shares.T, 0.0)
    all_panels = jnp.concatenate(factor_parts, axis=1)
    width = all_panels.shape[1] // col_count
    panel_factor = lax.dynamic_slice_in_dim(all_panels, lax.axis_index("col") * width, width, 1)
    return (panel_factor, sketch)


def solution(mesh):
    return jax.shard_map(
        per_device,
        mesh=mesh,
        in_specs=(
            P("row", "col"),
            P(("row", "col"), None),
            P(("row", "col")),
            P(("row", "col")),
            P("col", None),
        ),
        out_specs=(P("row", "col"), P("row", "col")),
        check_vma=False,
    )
```

profile of v0, /device:TPU:1, one launch (start us, length us, event | category | flops | bytes accessed | tf_op | source)
XLA Modules:
  0.0 1003.4 jit_solution(17757820655012956910)
XLA Ops:
  9.4 2.6 fusion.101
  11.9 2.6 fusion.129
  17.6 11.5 %all-to-all-start = ((s32[128,1,2]{2,1,0:T(1,128)}), s32[128,1,2]{2,1,0:T(1,128)S(1)}, u32[]{:S(2)}, u32[]{:S(2)}) async-start(s32[128,1,2]{2,1,0:T(1,128)} %bitcast.16), calls=%async_computation | async-start | bytes 131072 | tf_op jit(solution)/shard_map/all_to_all | solution.py:30
  29.1 1.9 copy.34
  32.3 2.2 pad_maximum_fusion
  34.5 5.7 copy.35
  40.1 6.8 scatter_custom_fusion.1
  46.9 4.6 slice.127
  51.5 5.8 reshape_transpose_transpose_reshape_reshape_reshape.7
  57.4 10.2 %all-to-all-start.1 = ((f32[128,1,2,4096]{3,2,1,0:T(2,128)}), f32[128,1,2,4096]{3,2,1,0:T(2,128)}, u32[]{:S(2)}, u32[]{:S(2)}) async-start(f32[128,1,2,4096]{3,2,1,0:T(2,128)} %bitcast.188), calls=%async_computation.1 | async-start | bytes 8388608 | tf_op jit(solution)/shard_map/all_to_all | solution.py:30
  68.0 52.1 %all-to-all-done.1 = f32[128,1,2,4096]{3,2,1,0:T(2,128)} async-done(((f32[128,1,2,4096]{3,2,1,0:T(2,128)}), f32[128,1,2,4096]{3,2,1,0:T(2,128)}, u32[]{:S(2)}, u32[]{:S(2)}) %all-to-all-start.1) | async-done | bytes 4194336 | tf_op jit(solution)/shard_map/all_to_all | solution.py:30
  120.1 6.0 reshape.543
  126.1 8.4 scatter_custom_fusion.2
  134.5 4.4 reshape.487
  138.9 8.6 copy.37
  147.5 6.2 reshape.488
  153.7 2.8 add.248
  157.8 27.1 %reduce-scatter.3.cloned.1.call-done = f32[72,512]{1,0:T(8,128)} async-done(((f32[576,512]{1,0:T(8,128)}), f32[72,512]{1,0:T(8,128)}) %reduce-scatter.3.cloned.1.call-update) | async-done | bytes 147472 | tf_op jit(solution)/shard_map/reduce_scatter | solution.py:47
  184.9 27.1 %all-gather.3.cloned.1.call-done = f32[576,512]{1,0:T(8,128)} async-done(((f32[72,512]{1,0:T(8,128)}), f32[576,512]{1,0:T(8,128)}) %all-gather.3.cloned.1.call-update) | async-done | bytes 1179664 | tf_op jit(solution)/shard_map/all_gather | solution.py:48
  213.1 2.9 fusion.17
  216.5 84.9 %all-reduce.8.cloned.1.call-done = f32[512,512]{1,0:T(8,128)} async-done(((f32[512,512]{1,0:T(8,128)}), f32[512,512]{1,0:T(8,128)}) %all-reduce.8.cloned.1.call-update) | async-done | bytes 1048592 | tf_op jit(solution)/shard_map/psum | solution.py:128
  301.4 2.5 copy.38
  304.0 2.7 fusion.20
  306.7 2.6 copy.39
  309.3 1.8 fusion.19
  312.1 11.7 %cholesky.286 = f32[128,128]{1,0:T(8,128)S(1)} custom-call(f32[128,128]{1,0:T(8,128)S(1)} %cholesky.426), custom_call_target="Cholesky" | custom-call | tf_op jit(solution)/shard_map/jit(cholesky)/cholesky | solution.py:129
  325.0 9.8 custom-call.27
  334.8 1.9 constant_dynamic-update-slice_fusion.1
  338.0 11.7 %cholesky.305 = f32[128,128]{1,0:T(8,128)S(1)} custom-call(f32[128,128]{1,0:T(8,128)S(1)} %cholesky.430), custom_call_target="Cholesky" | custom-call | tf_op jit(solution)/shard_map/jit(cholesky)/cholesky | solution.py:129
  350.4 10.0 custom-call.28
  362.7 11.7 %cholesky.326 = f32[128,128]{1,0:T(8,128)S(1)} custom-call(f32[128,128]{1,0:T(8,128)S(1)} %cholesky.435), custom_call_target="Cholesky" | custom-call | tf_op jit(solution)/shard_map/jit(cholesky)/cholesky | solution.py:129
  375.7 9.8 custom-call.29
  387.8 12.1 %cholesky.343 = f32[128,128]{1,0:T(8,128)S(1)} custom-call(f32[128,128]{1,0:T(8,128)S(1)} %convolution_subtract_fusion.13), custom_call_target="Cholesky" | custom-call | tf_op jit(solution)/shard_map/jit(cholesky)/cholesky | solution.py:129
  404.4 2.4 select_select_fusion.1
  406.8 11.9 %while.4 = (s32[]{:T(128)}, f32[512,512]{1,0:T(8,128)}, s32[4,2]{0,1:T(2,128)S(1)}, f32[4,128,128]{2,1,0:T(8,128)S(1)}, s32[]{:T(128)}) while((s32[]{:T(128)}, f32[512,512]{1,0:T(8,128)}, s32[4,2]{0,1:T(2,128)S(1)}, f32[4,128,128]{2,1,0:T(8,128)S(1)}, s32[]{:T(128)}) %tuple.68), condition=%wide.while_cond, body=%wide.while_body.sunk | while | flops 2 | bytes 131181 | solution.py:130
  407.5 2.3 bitcast_dynamic-update-slice_fusion.4
  410.5 2.3 bitcast_dynamic-update-slice_fusion.4
  413.5 2.3 bitcast_dynamic-update-slice_fusion.4
  416.5 2.3 bitcast_dynamic-update-slice_fusion.4
  418.8 39.3 %custom-call.30 = f32[4,128,128]{1,2,0:T(8,128)S(1)} custom-call(f32[4,128,128]{2,1,0:T(8,128)S(1)} %get-tuple-element.18), custom_call_target="InvertDiagBlocksLowerTriangular" | custom-call | tf_op jit(solution)/shard_map/jit(_solve_triangular)/triangular_solve | solution.py:130
  464.2 1.9 convolution_subtract_fusion.7
  467.3 2.1 select_bitcast_fusion.4
  469.5 91.7 %all-reduce.14.cloned.1.call-done = (f32[576,512]{1,0:T(8,128)}, f32[576,512]{1,0:T(8,128)}) async-done(((f32[576,512]{1,0:T(8,128)}, f32[576,512]{1,0:T(8,128)}), (f32[576,512]{1,0:T(8,128)}, f32[576,512]{1,0:T(8,128)})) %all-reduce.14.cloned.1.call-update) | async-done | bytes 2359312 | tf_op jit(solution)/shard_map/psum | solution.py:53
  561.2 6.9 convolution_subtract_fusion.1
  570.8 30.4 %reduce-scatter.5.cloned.1.call-done = f32[72,512]{1,0:T(8,128)} async-done(((f32[576,512]{1,0:T(8,128)}), f32[72,512]{1,0:T(8,128)}) %reduce-scatter.5.cloned.1.call-update) | async-done | bytes 147472 | tf_op jit(solution)/shard_map/reduce_scatter | solution.py:47
  601.3 26.9 %all-gather.5.cloned.1.call-done = f32[576,512]{1,0:T(8,128)} async-done(((f32[72,512]{1,0:T(8,128)}), f32[576,512]{1,0:T(8,128)}) %all-gather.5.cloned.1.call-update) | async-done | bytes 1179664 | tf_op jit(solution)/shard_map/all_gather | solution.py:48
  628.2 2.6 fusion.15
  631.0 86.2 %all-reduce.10.cloned.1.call-done = f32[512,512]{1,0:T(8,128)} async-done(((f32[512,512]{1,0:T(8,128)}), f32[512,512]{1,0:T(8,128)}) %all-reduce.10.cloned.1.call-update) | async-done | bytes 1048592 | tf_op jit(solution)/shard_map/psum | solution.py:128
  720.1 11.7 %cholesky.358 = f32[128,128]{1,0:T(8,128)S(1)} custom-call(f32[128,128]{1,0:T(8,128)S(1)} %cholesky.439), custom_call_target="Cholesky" | custom-call | tf_op jit(solution)/shard_map/jit(cholesky)/cholesky | solution.py:129
  732.0 9.8 custom-call.31
  742.5 11.7 %cholesky.377 = f32[128,128]{1,0:T(8,128)S(1)} custom-call(f32[128,128]{1,0:T(8,128)S(1)} %cholesky.443), custom_call_target="Cholesky" | custom-call | tf_op jit(solution)/shard_map/jit(cholesky)/cholesky | solution.py:129
  755.5 10.2 %custom-call.32 = f32[1,128,128]{1,2,0:T(8,128)S(1)} custom-call(f32[1,128,128]{2,1,0:T(8,128)S(1)} %get-tuple-element.58), custom_call_target="InvertDiagBlocksLowerTriangular" | custom-call | tf_op jit(solution)/shard_map/jit(cholesky)/cholesky | solution.py:129
  766.4 11.7 %cholesky.398 = f32[128,128]{1,0:T(8,128)S(1)} custom-call(f32[128,128]{1,0:T(8,128)S(1)} %cholesky.448), custom_call_target="Cholesky" | custom-call | tf_op jit(solution)/shard_map/jit(cholesky)/cholesky | solution.py:129
  778.7 9.8 custom-call.33
  789.2 11.9 %cholesky.415 = f32[128,128]{1,0:T(8,128)S(1)} custom-call(f32[128,128]{1,0:T(8,128)S(1)} %convolution_subtract_fusion.12), custom_call_target="Cholesky" | custom-call | tf_op jit(solution)/shard_map/jit(cholesky)/cholesky | solution.py:129
  804.4 7.7 while.5
  812.1 39.3 %custom-call.34 = f32[4,128,128]{1,2,0:T(8,128)S(1)} custom-call(f32[4,128,128]{2,1,0:T(8,128)S(1)} %get-tuple-element.19), custom_call_target="InvertDiagBlocksLowerTriangular" | custom-call | tf_op jit(solution)/shard_map/jit(_solve_triangular)/triangular_solve | solution.py:130
  855.4 1.8 convolution_subtract_fusion.6
  857.7 2.1 select_bitcast_fusion.1
  859.8 91.7 %all-reduce.12.cloned.1.call-done = (f32[576,512]{1,0:T(8,128)}, f32[576,512]{1,0:T(8,128)}) async-done(((f32[576,512]{1,0:T(8,128)}, f32[576,512]{1,0:T(8,128)}), (f32[576,512]{1,0:T(8,128)}, f32[576,512]{1,0:T(8,128)})) %all-reduce.12.cloned.1.call-update) | async-done | bytes 2359312 | tf_op jit(solution)/shard_map/psum | solution.py:53
  951.6 7.0 convolution_subtract_fusion
  958.6 12.7 %fusion.6 = f32[512,576]{1,0:T(8,128)} fusion(f32[576,1152]{1,0:T(8,128)S(1)} %convolution_subtract_fusion, f32[1152,512]{1,0:T(8,128)S(1)} %copy-done.12, pred[1152]{0:T(1024)(128)(4,1)S(1)} %add_compare_fusion), kind=kOutput, calls=%fused_computation.24 | convolution fusion | flops 4077453312 | bytes 6194304 | tf_op jit(solution)/shard_map/dot_general | solution.py:141
  971.3 6.5 all-to-all-start.2
  978.6 17.0 %all-to-all-done.2 = f32[8,64,576]{2,1,0:T(8,128)S(1)} async-done(((f32[8,64,576]{2,1,0:T(8,128)}), f32[8,64,576]{2,1,0:T(8,128)S(1)}, u32[]{:S(2)}, u32[]{:S(2)}) %all-to-all-start.2) | async-done | bytes 1179680 | tf_op jit(solution)/shard_map/all_to_all | solution.py:58
  (155 shorter events, 56.0 us)
Async XLA Ops:
  17.6 39.7 %all-to-all-start = ((s32[128,1,2]{2,1,0:T(1,128)}), s32[128,1,2]{2,1,0:T(1,128)S(1)}, u32[]{:S(2)}, u32[]{:S(2)}) async-start(s32[128,1,2]{2,1,0:T(1,128)} %bitcast.16), calls=%async_computation | async-start | bytes 131072 | tf_op jit(solution)/shard_map/all_to_all | solution.py:30
  57.4 62.7 %all-to-all-start.1 = ((f32[128,1,2,4096]{3,2,1,0:T(2,128)}), f32[128,1,2,4096]{3,2,1,0:T(2,128)}, u32[]{:S(2)}, u32[]{:S(2)}) async-start(f32[128,1,2,4096]{3,2,1,0:T(2,128)} %bitcast.188), calls=%async_computation.1 | async-start | bytes 8388608 | tf_op jit(solution)/shard_map/all_to_all | solution.py:30
  67.6 117.3 %reduce-scatter.3.cloned.1.call-start = ((), (), s32[]{:S(2)}) async-start(), calls=%async_computation.5 | async-start | bytes 1327104 | tf_op jit(solution)/shard_map/reduce_scatter | solution.py:47
  157.7 54.3 %all-gather.3.cloned.1.call-start = ((), (), s32[]{:S(2)}) async-start(), calls=%async_computation.6 | async-start | bytes 1327104 | tf_op jit(solution)/shard_map/all_gather | solution.py:48
  184.9 116.6 %all-reduce.8.cloned.1.call-start = ((), (), s32[]{:S(2)}) async-start(), calls=%async_computation.7 | async-start | bytes 2097152 | tf_op jit(solution)/shard_map/psum | solution.py:128
  212.1 1.0 copy-start.2
  216.0 345.1 %all-reduce.14.cloned.1.call-start = ((), (), s32[]{:S(2)}) async-start(), calls=%async_computation.12 | async-start | bytes 4718592 | tf_op jit(solution)/shard_map/psum | solution.py:53
  311.1 1.0 copy-start.9
  458.1 3.3 copy-start.13
  458.1 3.3 copy-start.4
  467.3 2.1 copy-start.11
  469.4 131.8 %reduce-scatter.5.cloned.1.call-start = ((), (), s32[]{:S(2)}) async-start(), calls=%async_computation.8 | async-start | bytes 1327104 | tf_op jit(solution)/shard_map/reduce_scatter | solution.py:47
  568.0 1.5 copy-start
  570.7 57.5 %copy-start.3 = (f32[512,512]{1,0:T(8,128)S(1)}, f32[512,512]{1,0:T(8,128)}, u32[]{:S(2)}) copy-start(f32[512,512]{1,0:T(8,128)} %copy-done.2) | copy-start | bytes 3145732
  570.8 57.4 %all-gather.5.cloned.1.call-start = ((), (), s32[]{:S(2)}) async-start(), calls=%async_computation.9 | async-start | bytes 1327104 | tf_op jit(solution)/shard_map/all_gather | solution.py:48
  601.3 116.0 %all-reduce.10.cloned.1.call-start = ((), (), s32[]{:S(2)}) async-start(), calls=%async_computation.10 | async-start | bytes 2097152 | tf_op jit(solution)/shard_map/psum | solution.py:128
  630.8 320.8 %all-reduce.12.cloned.1.call-start = ((), (), s32[]{:S(2)}) async-start(), calls=%async_computation.11 | async-start | bytes 4718592 | tf_op jit(solution)/shard_map/psum | solution.py:53
  717.2 1.7 copy-start.7
  804.3 47.2 %copy-start.5 = (f32[576,512]{1,0:T(8,128)S(1)}, f32[576,512]{1,0:T(8,128)}, u32[]{:S(2)}) copy-start(f32[576,512]{1,0:T(8,128)} %all-gather.5.cloned.1.call-done) | copy-start | bytes 3538948
  812.1 39.3 %copy-start.8 = (f32[512,512]{1,0:T(8,128)}, f32[512,512]{1,0:T(8,128)S(1)}, u32[]{:S(2)}) copy-start(f32[512,512]{1,0:T(8,128)S(1)} %get-tuple-element.216) | copy-start | bytes 3145732
  857.6 2.1 copy-start.10
  857.7 93.9 %copy-start.1 = (f32[576,1152]{1,0:T(8,128)S(1)}, f32[576,1152]{1,0:T(8,128)}, u32[]{:S(2)}) copy-start(f32[576,1152]{1,0:T(8,128)} %copy-done) | copy-start | bytes 7962628
  951.6 7.0 copy-start.12
  971.3 6.5 copy-start.6
  971.3 24.3 %all-to-all-start.2 = ((f32[8,64,576]{2,1,0:T(8,128)}), f32[8,64,576]{2,1,0:T(8,128)S(1)}, u32[]{:S(2)}, u32[]{:S(2)}) async-start(f32[8,64,576]{2,1,0:T(8,128)} %bitcast.63), calls=%async_computation.4 | async-start | bytes 2621440 | tf_op jit(solution)/shard_map/all_to_all | solution.py:58
Sparse Core Ops, SparseCore 0:
  157.8 26.9 reduce-scatter.2
  186.5 25.4 all-gather.2
  216.2 85.2 all-reduce.7
  469.5 91.5 all-reduce.13
  570.9 30.2 reduce-scatter.4
  602.8 25.3 all-gather.4
  631.4 85.7 all-reduce.9
  859.9 91.6 all-reduce.11
where the time goes:
time: 1010 us; the launch traced here: 1000 us
  waiting for transfers between devices  535 us (53%)
  other arithmetic  280 us (28%)
  local copies, waits for them, and re-layouts  87.2 us (9%)
  matrix products  51.5 us (5%)
  starting transfers between devices  29.3 us (3%)
  between operations  20 us (2%)
    psum x2, waiting for transfers between devices, broadcast(): return lax.psum(jnp.where(mine, value, jnp.zeros_like(value)), axis)  183 us
    psum x2, waiting for transfers between devices, per_device(): diag_block = lax.psum(piece, 'row')  171 us
    another operation x29, other arithmetic, per_device(): chol = jnp.linalg.cholesky(0.5 * (diag_block + diag_block.T))  160 us
    another operation x5, other arithmetic, per_device(): solved = jax.scipy.linalg.solve_triangular(chol, panel.T, lower=True).T  81.2 us
    reduce_scatter x2, waiting for transfers between devices, from_root(): own = lax.psum_scatter(padded, axis, scatter_dimension=0, tiled=True)  57.5 us
    all_gather x2, waiting for transfers between devices, from_root(): lax.all_gather(own, axis, axis=0, tiled=True)[:len(lines)]  53.9 us
    all_to_all x2, waiting for transfers between devices, one_exchange(): tiles = lax.all_to_all(tiles, axis, split_axis=0, concat_axis=0, tiled=True)  52.1 us
    all_to_all x2, starting transfers between devices, one_exchange(): tiles = lax.all_to_all(tiles, axis, split_axis=0, concat_axis=0, tiled=True)  21.7 us
  transfers between devices with their start and end apart: 11, of which 10 were waited for; matrix products, arithmetic and copies ran while one was open for 3% of the time, Pallas kernels for 0%

commit v1 on v0

--- a/solution.py
+++ b/solution.py
@@ -125,7 +125,7 @@
         padded = jnp.concatenate([margin, panel, margin], axis=0)
         begin = jnp.clip(low - row_start + NB, 0, local_rows + NB)
         piece = lax.dynamic_slice_in_dim(padded, begin, NB, 0)
-        diag_block = lax.psum(piece, "row")
+        diag_block = jnp.sum(lax.all_gather(piece, "row"), axis=0)
         chol = jnp.linalg.cholesky(0.5 * (diag_block + diag_block.T))
         solved = jax.scipy.linalg.solve_triangular(chol, panel.T, lower=True).T
         factor_parts.append(jnp.where((global_rows >= low)[:, None], solved, 0.0))

time: 1010 us -> 1080 us (1.069)
  waiting for transfers between devices: 535 us -> 583 us
  other arithmetic: 280 us -> 297 us
    all_gather x0 -> x2, waiting for transfers between devices: none -> 221 us  [per_device(): diag_block = jnp.sum(lax.all_gather(piece, 'row'), axis=0)]
    psum x2 -> x0, waiting for transfers between devices: 171 us -> none  [per_device(): diag_block = lax.psum(piece, 'row')]
    reduce_sum x0 -> x2, other arithmetic: none -> 16.9 us  [per_device(): diag_block = jnp.sum(lax.all_gather(piece, 'row'), axis=0)]
where the time goes in v1:
time: 1080 us; the launch traced here: 1070 us
  waiting for transfers between devices  583 us (54%)
  other arithmetic  297 us (28%)
  local copies, waits for them, and re-layouts  86.3 us (8%)
  matrix products  51.5 us (5%)
  starting transfers between devices  29.3 us (3%)
  between operations  20.2 us (2%)
    all_gather x2, waiting for transfers between devices, per_device(): diag_block = jnp.sum(lax.all_gather(piece, 'row'), axis=0)  221 us
    psum x2, waiting for transfers between devices, broadcast(): return lax.psum(jnp.where(mine, value, jnp.zeros_like(value)), axis)  182 us
    another operation x29, other arithmetic, per_device(): chol = jnp.linalg.cholesky(0.5 * (diag_block + diag_block.T))  160 us
    another operation x5, other arithmetic, per_device(): solved = jax.scipy.linalg.solve_triangular(chol, panel.T, lower=True).T  81.2 us
    reduce_scatter x2, waiting for transfers between devices, from_root(): own = lax.psum_scatter(padded, axis, scatter_dimension=0, tiled=True)  57.5 us
    all_gather x2, waiting for transfers between devices, from_root(): lax.all_gather(own, axis, axis=0, tiled=True)[:len(lines)]  53.9 us
    all_to_all x2, waiting for transfers between devices, one_exchange(): tiles = lax.all_to_all(tiles, axis, split_axis=0, concat_axis=0, tiled=True)  52.1 us
    all_to_all x2, starting transfers between devices, one_exchange(): tiles = lax.all_to_all(tiles, axis, split_axis=0, concat_axis=0, tiled=True)  21.7 us
  transfers between devices with their start and end apart: 11, of which 10 were waited for; matrix products, arithmetic and copies ran while one was open for 3% of the time, Pallas kernels for 0%

profile of v1, /device:TPU:1, one launch (start us, length us, event | category | flops | bytes accessed | tf_op | source)
XLA Modules:
  0.0 1067.3 jit_solution(4312861428371530392)
XLA Ops:
  9.4 2.6 fusion.102
  11.9 2.6 fusion.130
  17.6 11.5 %all-to-all-start = ((s32[128,1,2]{2,1,0:T(1,128)}), s32[128,1,2]{2,1,0:T(1,128)S(1)}, u32[]{:S(2)}, u32[]{:S(2)}) async-start(s32[128,1,2]{2,1,0:T(1,128)} %bitcast.16), calls=%async_computation | async-start | bytes 131072 | tf_op jit(solution)/shard_map/all_to_all | solution.py:30
  29.1 1.9 copy.32
  32.3 2.2 pad_maximum_fusion
  34.5 5.7 copy.33
  40.1 6.8 scatter_custom_fusion.1
  46.9 4.6 slice.127
  51.5 5.8 reshape_transpose_transpose_reshape_reshape_reshape.7
  57.4 10.2 all-to-all-start.1
  68.0 52.1 %all-to-all-done.1 = f32[128,1,2,4096]{3,2,1,0:T(2,128)} async-done(((f32[128,1,2,4096]{3,2,1,0:T(2,128)}), f32[128,1,2,4096]{3,2,1,0:T(2,128)}, u32[]{:S(2)}, u32[]{:S(2)}) %all-to-all-start.1) | async-done | bytes 4194336 | tf_op jit(solution)/shard_map/all_to_all | solution.py:30
  120.1 6.0 reshape.543
  126.1 8.4 scatter_custom_fusion.2
  134.5 4.4 reshape.487
  138.9 8.6 copy.35
  147.5 6.2 reshape.488
  153.7 2.8 add.244
  157.8 27.1 %reduce-scatter.3.cloned.1.call-done = f32[72,512]{1,0:T(8,128)} async-done(((f32[576,512]{1,0:T(8,128)}), f32[72,512]{1,0:T(8,128)}) %reduce-scatter.3.cloned.1.call-update) | async-done | bytes 147472 | tf_op jit(solution)/shard_map/reduce_scatter | solution.py:47
  184.9 27.1 %all-gather.7.cloned.1.call-done = f32[576,512]{1,0:T(8,128)} async-done(((f32[72,512]{1,0:T(8,128)}), f32[576,512]{1,0:T(8,128)}) %all-gather.7.cloned.1.call-update) | async-done | bytes 1179664 | tf_op jit(solution)/shard_map/all_gather | solution.py:48
  213.1 3.0 fusion.17
  216.6 110.0 %all-gather.11.cloned.1.call-done = f32[8192,512]{1,0:T(8,128)} async-done(((f32[512,512]{1,0:T(8,128)}), f32[8192,512]{1,0:T(8,128)}) %all-gather.11.cloned.1.call-update) | async-done | bytes 16777232 | tf_op jit(solution)/shard_map/all_gather | solution.py:128
  326.6 8.9 reduce_sum.40
  335.5 2.6 copy.36
  338.1 2.8 fusion.21
  340.8 2.6 copy.37
  346.2 11.7 %cholesky.286 = f32[128,128]{1,0:T(8,128)S(1)} custom-call(f32[128,128]{1,0:T(8,128)S(1)} %cholesky.426), custom_call_target="Cholesky" | custom-call | tf_op jit(solution)/shard_map/jit(cholesky)/cholesky | solution.py:129
  359.1 9.8 custom-call.27
  368.9 2.0 constant_dynamic-update-slice_fusion.1
  372.2 11.9 %cholesky.305 = f32[128,128]{1,0:T(8,128)S(1)} custom-call(f32[128,128]{1,0:T(8,128)S(1)} %cholesky.430), custom_call_target="Cholesky" | custom-call | tf_op jit(solution)/shard_map/jit(cholesky)/cholesky | solution.py:129
  384.7 9.8 custom-call.28
  396.9 11.7 %cholesky.326 = f32[128,128]{1,0:T(8,128)S(1)} custom-call(f32[128,128]{1,0:T(8,128)S(1)} %cholesky.435), custom_call_target="Cholesky" | custom-call | tf_op jit(solution)/shard_map/jit(cholesky)/cholesky | solution.py:129
  409.9 9.8 custom-call.29
  422.0 12.1 %cholesky.343 = f32[128,128]{1,0:T(8,128)S(1)} custom-call(f32[128,128]{1,0:T(8,128)S(1)} %convolution_subtract_fusion.13), custom_call_target="Cholesky" | custom-call | tf_op jit(solution)/shard_map/jit(cholesky)/cholesky | solution.py:129
  438.6 2.4 select_select_fusion.1
  441.0 11.9 %while.4 = (s32[]{:T(128)}, f32[512,512]{1,0:T(8,128)}, s32[4,2]{0,1:T(2,128)S(1)}, f32[4,128,128]{2,1,0:T(8,128)S(1)}, s32[]{:T(128)}) while((s32[]{:T(128)}, f32[512,512]{1,0:T(8,128)}, s32[4,2]{0,1:T(2,128)S(1)}, f32[4,128,128]{2,1,0:T(8,128)S(1)}, s32[]{:T(128)}) %tuple.68), condition=%wide.while_cond, body=%wide.while_body.sunk | while | flops 2 | bytes 131181 | solution.py:130
  441.7 2.3 bitcast_dynamic-update-slice_fusion.4
  444.7 2.3 bitcast_dynamic-update-slice_fusion.4
  447.7 2.3 bitcast_dynamic-update-slice_fusion.4
  450.7 2.3 bitcast_dynamic-update-slice_fusion.4
  452.9 39.3 %custom-call.30 = f32[4,128,128]{1,2,0:T(8,128)S(1)} custom-call(f32[4,128,128]{2,1,0:T(8,128)S(1)} %get-tuple-element.18), custom_call_target="InvertDiagBlocksLowerTriangular" | custom-call | tf_op jit(solution)/shard_map/jit(_solve_triangular)/triangular_solve | solution.py:130
  498.4 1.9 convolution_subtract_fusion.7
  501.5 2.1 select_bitcast_fusion.4
  503.7 90.8 %all-reduce.8.cloned.1.call-done = (f32[576,512]{1,0:T(8,128)}, f32[576,512]{1,0:T(8,128)}) async-done(((f32[576,512]{1,0:T(8,128)}, f32[576,512]{1,0:T(8,128)}), (f32[576,512]{1,0:T(8,128)}, f32[576,512]{1,0:T(8,128)})) %all-reduce.8.cloned.1.call-update) | async-done | bytes 2359312 | tf_op jit(solution)/shard_map/psum | solution.py:53
  594.5 6.9 convolution_subtract_fusion.1
  604.1 30.4 %reduce-scatter.5.cloned.1.call-done = f32[72,512]{1,0:T(8,128)} async-done(((f32[576,512]{1,0:T(8,128)}), f32[72,512]{1,0:T(8,128)}) %reduce-scatter.5.cloned.1.call-update) | async-done | bytes 147472 | tf_op jit(solution)/shard_map/reduce_scatter | solution.py:47
  634.6 26.9 %all-gather.9.cloned.1.call-done = f32[576,512]{1,0:T(8,128)} async-done(((f32[72,512]{1,0:T(8,128)}), f32[576,512]{1,0:T(8,128)}) %all-gather.9.cloned.1.call-update) | async-done | bytes 1179664 | tf_op jit(solution)/shard_map/all_gather | solution.py:48
  661.5 2.6 fusion.15
  664.4 110.6 %all-gather.13.cloned.1.call-done = f32[8192,512]{1,0:T(8,128)} async-done(((f32[512,512]{1,0:T(8,128)}), f32[8192,512]{1,0:T(8,128)}) %all-gather.13.cloned.1.call-update) | async-done | bytes 16777232 | tf_op jit(solution)/shard_map/all_gather | solution.py:128
  774.9 7.9 reduce_sum.41
  784.0 11.7 %cholesky.358 = f32[128,128]{1,0:T(8,128)S(1)} custom-call(f32[128,128]{1,0:T(8,128)S(1)} %cholesky.439), custom_call_target="Cholesky" | custom-call | tf_op jit(solution)/shard_map/jit(cholesky)/cholesky | solution.py:129
  795.9 9.8 custom-call.31
  806.4 12.1 %cholesky.377 = f32[128,128]{1,0:T(8,128)S(1)} custom-call(f32[128,128]{1,0:T(8,128)S(1)} %cholesky.443), custom_call_target="Cholesky" | custom-call | tf_op jit(solution)/shard_map/jit(cholesky)/cholesky | solution.py:129
  819.9 9.8 custom-call.32
  830.3 11.7 %cholesky.398 = f32[128,128]{1,0:T(8,128)S(1)} custom-call(f32[128,128]{1,0:T(8,128)S(1)} %cholesky.448), custom_call_target="Cholesky" | custom-call | tf_op jit(solution)/shard_map/jit(cholesky)/cholesky | solution.py:129
  842.7 9.8 custom-call.33
  853.1 11.9 %cholesky.415 = f32[128,128]{1,0:T(8,128)S(1)} custom-call(f32[128,128]{1,0:T(8,128)S(1)} %convolution_subtract_fusion.12), custom_call_target="Cholesky" | custom-call | tf_op jit(solution)/shard_map/jit(cholesky)/cholesky | solution.py:129
  868.4 8.5 while.5
  876.9 39.3 %custom-call.34 = f32[4,128,128]{1,2,0:T(8,128)S(1)} custom-call(f32[4,128,128]{2,1,0:T(8,128)S(1)} %get-tuple-element.19), custom_call_target="InvertDiagBlocksLowerTriangular" | custom-call | tf_op jit(solution)/shard_map/jit(_solve_triangular)/triangular_solve | solution.py:130
  922.5 2.1 select_bitcast_fusion.1
  924.6 90.8 %all-reduce.6.cloned.1.call-done = (f32[576,512]{1,0:T(8,128)}, f32[576,512]{1,0:T(8,128)}) async-done(((f32[576,512]{1,0:T(8,128)}, f32[576,512]{1,0:T(8,128)}), (f32[576,512]{1,0:T(8,128)}, f32[576,512]{1,0:T(8,128)})) %all-reduce.6.cloned.1.call-update) | async-done | bytes 2359312 | tf_op jit(solution)/shard_map/psum | solution.py:53
  1015.4 7.0 convolution_subtract_fusion
  1022.5 12.7 %fusion.6 = f32[512,576]{1,0:T(8,128)} fusion(f32[576,1152]{1,0:T(8,128)S(1)} %convolution_subtract_fusion, f32[1152,512]{1,0:T(8,128)S(1)} %copy-done.11, pred[1152]{0:T(1024)(128)(4,1)S(1)} %add_compare_fusion), kind=kOutput, calls=%fused_computation.24 | convolution fusion | flops 4077453312 | bytes 6194304 | tf_op jit(solution)/shard_map/dot_general | solution.py:141
  1035.1 6.5 all-to-all-start.2
  1042.4 17.0 %all-to-all-done.2 = f32[8,64,576]{2,1,0:T(8,128)S(1)} async-done(((f32[8,64,576]{2,1,0:T(8,128)}), f32[8,64,576]{2,1,0:T(8,128)S(1)}, u32[]{:S(2)}, u32[]{:S(2)}) %all-to-all-start.2) | async-done | bytes 1179680 | tf_op jit(solution)/shard_map/all_to_all | solution.py:58
  (153 shorter events, 58.7 us)
Async XLA Ops:
  17.6 39.7 %all-to-all-start = ((s32[128,1,2]{2,1,0:T(1,128)}), s32[128,1,2]{2,1,0:T(1,128)S(1)}, u32[]{:S(2)}, u32[]{:S(2)}) async-start(s32[128,1,2]{2,1,0:T(1,128)} %bitcast.16), calls=%async_computation | async-start | bytes 131072 | tf_op jit(solution)/shard_map/all_to_all | solution.py:30
  57.4 62.7 %all-to-all-start.1 = ((f32[128,1,2,4096]{3,2,1,0:T(2,128)}), f32[128,1,2,4096]{3,2,1,0:T(2,128)}, u32[]{:S(2)}, u32[]{:S(2)}) async-start(f32[128,1,2,4096]{3,2,1,0:T(2,128)} %bitcast.194), calls=%async_computation.1 | async-start | bytes 8388608 | tf_op jit(solution)/shard_map/all_to_all | solution.py:30
  67.6 117.3 %reduce-scatter.3.cloned.1.call-start = ((), (), s32[]{:S(2)}) async-start(), calls=%async_computation.5 | async-start | bytes 1327104 | tf_op jit(solution)/shard_map/reduce_scatter | solution.py:47
  157.7 54.3 %all-gather.7.cloned.1.call-start = ((), (), s32[]{:S(2)}) async-start(), calls=%async_computation.6 | async-start | bytes 1327104 | tf_op jit(solution)/shard_map/all_gather | solution.py:48
  184.9 141.7 %all-gather.11.cloned.1.call-start = ((), (), s32[]{:S(2)}) async-start(), calls=%async_computation.9 | async-start | bytes 17825792 | tf_op jit(solution)/shard_map/all_gather | solution.py:128
  212.1 1.0 copy-start.2
  216.1 378.4 %all-reduce.8.cloned.1.call-start = ((), (), s32[]{:S(2)}) async-start(), calls=%async_computation.12 | async-start | bytes 4718592 | tf_op jit(solution)/shard_map/psum | solution.py:53
  345.2 1.0 copy-start.8
  492.3 3.3 copy-start.12
  492.3 3.3 copy-start.4
  501.5 2.1 copy-start.10
  503.6 130.9 %reduce-scatter.5.cloned.1.call-start = ((), (), s32[]{:S(2)}) async-start(), calls=%async_computation.7 | async-start | bytes 1327104 | tf_op jit(solution)/shard_map/reduce_scatter | solution.py:47
  601.3 1.5 copy-start
  604.0 57.5 %copy-start.3 = (f32[512,512]{1,0:T(8,128)S(1)}, f32[512,512]{1,0:T(8,128)}, u32[]{:S(2)}) copy-start(f32[512,512]{1,0:T(8,128)} %copy-done.2) | copy-start | bytes 3145732
  604.1 57.4 %all-gather.9.cloned.1.call-start = ((), (), s32[]{:S(2)}) async-start(), calls=%async_computation.8 | async-start | bytes 1327104 | tf_op jit(solution)/shard_map/all_gather | solution.py:48
  634.5 140.4 %all-gather.13.cloned.1.call-start = ((), (), s32[]{:S(2)}) async-start(), calls=%async_computation.10 | async-start | bytes 17825792 | tf_op jit(solution)/shard_map/all_gather | solution.py:128
  664.1 351.3 %all-reduce.6.cloned.1.call-start = ((), (), s32[]{:S(2)}) async-start(), calls=%async_computation.11 | async-start | bytes 4718592 | tf_op jit(solution)/shard_map/psum | solution.py:53
  868.2 48.0 %copy-start.5 = (f32[576,512]{1,0:T(8,128)S(1)}, f32[576,512]{1,0:T(8,128)}, u32[]{:S(2)}) copy-start(f32[576,512]{1,0:T(8,128)} %all-gather.9.cloned.1.call-done) | copy-start | bytes 3538948
  876.9 39.3 %copy-start.7 = (f32[512,512]{1,0:T(8,128)}, f32[512,512]{1,0:T(8,128)S(1)}, u32[]{:S(2)}) copy-start(f32[512,512]{1,0:T(8,128)S(1)} %get-tuple-element.216) | copy-start | bytes 3145732
  922.4 2.1 copy-start.9
  922.5 93.0 %copy-start.1 = (f32[576,1152]{1,0:T(8,128)S(1)}, f32[576,1152]{1,0:T(8,128)}, u32[]{:S(2)}) copy-start(f32[576,1152]{1,0:T(8,128)} %copy-done) | copy-start | bytes 7962628
  1015.4 7.0 copy-start.11
  1035.1 6.5 copy-start.6
  1035.1 24.3 %all-to-all-start.2 = ((f32[8,64,576]{2,1,0:T(8,128)}), f32[8,64,576]{2,1,0:T(8,128)S(1)}, u32[]{:S(2)}, u32[]{:S(2)}) async-start(f32[8,64,576]{2,1,0:T(8,128)} %bitcast.65), calls=%async_computation.4 | async-start | bytes 2621440 | tf_op jit(solution)/shard_map/all_to_all | solution.py:58
Sparse Core Ops, SparseCore 0:
  157.8 26.9 reduce-scatter.2
  186.5 25.4 all-gather.6
  216.2 110.3 all-gather.10
  503.7 90.6 all-reduce.7
  604.2 30.2 reduce-scatter.4
  636.1 25.3 all-gather.8
  664.2 110.6 all-gather.12
  924.7 90.6 all-reduce.5
